TPU v7x, 16 devices: a whole 2x2x2 slice. The times are simulated.
16 devices in a mesh: dz: 2 (over z), dy: 2 (over y), dx: 4 (over x, core).
Axes of the slice: x: 2, y: 2, z: 2, core: 2. Of those that a mesh axis runs over, the one named last changes fastest.
Arguments:
- act_one: bfloat16 [32768, 768], P(('dz', 'dy', 'dx'))
- pre_one: bfloat16 [32768, 3072], P(('dz', 'dy', 'dx'))
- act_two: bfloat16 [32768, 768], P(('dz', 'dy', 'dx'))
- pre_two: bfloat16 [32768, 3072], P(('dz', 'dy', 'dx'))
- grad_out: bfloat16 [32768, 768], P(('dz', 'dy', 'dx'))
- w_in_two: bfloat16 [768, 3072], replicated
- w_out_one: bfloat16 [3072, 768], replicated
- w_out_two: bfloat16 [3072, 768], replicated
Outputs:
- output: float32 [9437184], P(('dx', 'dy', 'dz'))
All inputs are finite; a program needn't handle non-finite values.
Results may differ from a plain program's by a relative error of at most 0.00159.
Values are sent between devices in bfloat16 or wider.
A program may use at most 1 GiB of HBM per device.

v0:
```python
import jax
import jax.numpy as jnp
from jax import lax
from jax.sharding import PartitionSpec as P, NamedSharding

N_MICRO = 2


def gelu_pair(pre):
    pre_wide = pre.astype(jnp.float32)
    hidden, pull_back = jax.vjp(jax.nn.gelu, pre_wide)
    return hidden, pull_back(jnp.ones_like(pre_wide))[0]


def local_grads(act_one, pre_one, act_two, pre_two, grad_out, w_in_two, w_out_one, w_out_two):
    hid_two, slope_two = gelu_pair(pre_two)
    hid_two = hid_two.astype(jnp.bfloat16)
    g_out_two = jnp.einsum('mtf,mtd->mfd', hid_two, grad_out, preferred_element_type=jnp.float32).astype(jnp.bfloat16)
    d_hid_two = jnp.einsum('mtd,fd->mtf', grad_out, w_out_two, preferred_element_type=jnp.float32)
    d_pre_two = (d_hid_two * slope_two).astype(jnp.bfloat16)
    g_in_two = jnp.einsum('mtd,mtf->mdf', act_two, d_pre_two, preferred_element_type=jnp.float32).astype(jnp.bfloat16)
    d_back_two = jnp.einsum('mtf,df->mtd', d_pre_two, w_in_two, preferred_element_type=jnp.float32)
    d_act_two = (grad_out.astype(jnp.float32) + d_back_two).astype(jnp.bfloat16)
    hid_one, slope_one = gelu_pair(pre_one)
    hid_one = hid_one.astype(jnp.bfloat16)
    g_out_one = jnp.einsum('mtf,mtd->mfd', hid_one, d_act_two, preferred_element_type=jnp.float32).astype(jnp.bfloat16)
    d_hid_one = jnp.einsum('mtd,fd->mtf', d_act_two, w_out_one, preferred_element_type=jnp.float32)
    d_pre_one = (d_hid_one * slope_one).astype(jnp.bfloat16)
    g_in_one = jnp.einsum('mtd,mtf->mdf', act_one, d_pre_one, preferred_element_type=jnp.float32).astype(jnp.bfloat16)
    batch_count = act_one.shape[0]
    return jnp.concatenate([grad_piece.reshape(batch_count, -1) for grad_piece in (g_out_two, g_in_two, g_out_one, g_in_one)], axis=1)


def solution(mesh):
    group_size = mesh.shape['dx']
    row_spec = P(('dz', 'dy', 'dx'), None)
    full_spec = P(None, None)

    def per_device(act_one, pre_one, act_two, pre_two, grad_out, w_in_two, w_out_one, w_out_two):
        micro_rows = act_one.shape[0] // N_MICRO
        split_rows = [array_in.reshape(N_MICRO, micro_rows, array_in.shape[1]) for array_in in (act_one, pre_one, act_two, pre_two, grad_out)]
        grad_rows = local_grads(*split_rows, w_in_two, w_out_one, w_out_two)
        total_len = grad_rows.shape[1]
        outgoing = grad_rows.reshape(N_MICRO, group_size, total_len // group_size)
        incoming = lax.all_to_all(outgoing, 'dx', 1, 1, tiled=True)
        part_sum = jnp.sum(incoming, axis=(0, 1), dtype=jnp.float32)
        part_sum = lax.psum_scatter(part_sum, 'dy', scatter_dimension=0, tiled=True)
        return lax.psum_scatter(part_sum, 'dz', scatter_dimension=0, tiled=True)

    return jax.shard_map(per_device, mesh=mesh, in_specs=(row_spec,) * 5 + (full_spec,) * 3, out_specs=P(('dx', 'dy', 'dz')), check_vma=False)
```

profile of v0, /device:TPU:0, one launch (start us, length us, event | category | flops | bytes accessed | tf_op | source)
XLA Modules:
  0.0 1178.5 jit_solution(11914548046352331668)
XLA Ops:
  6.5 0.0 copy-start
  6.5 0.0 all-reduce.5.cloned.1.call-start
  6.5 0.0 copy-start.2
  6.5 23.0 %fusion.30 = bf16[2,3072,768]{2,1,0:T(8,128)(2,1)} fusion(bf16[2,1024,768]{2,1,0:T(8,128)(2,1)} %bitcast.38, bf16[2,1024,3072]{2,1,0:T(8,128)(2,1)} %bitcast.34), kind=kOutput, calls=%fused_computation.38 | convolution fusion | flops 9731309568 | bytes 25165824 | tf_op jit(solution)/shard_map/mtf,mtd->mfd/dot_general | solution.py:18
  29.5 0.0 copy-done.2
  29.6 0.0 copy-start.3
  29.6 0.0 copy-start.4
  29.6 29.5 %fusion.9 = bf16[2,1024,3072]{2,1,0:T(8,128)(2,1)} fusion(bf16[2,1024,3072]{2,1,0:T(8,128)(2,1)} %bitcast.35, bf16[2,1024,768]{2,1,0:T(8,128)(2,1)} %bitcast.39, bf16[3072,768]{1,0:T(8,128)(2,1)S(1)} %copy-done.2), kind=kOutput, calls=%fused_computation.21 | convolution fusion | flops 9789505536 | bytes 33030144 | tf_op jit(solution)/shard_map/mtd,fd->mtf/dot_general | solution.py:19
  59.1 0.0 copy-done.3
  59.1 0.0 copy-done.4
  59.1 13.0 %add_convert_fusion = bf16[2,1024,768]{2,1,0:T(8,128)(2,1)S(1)} fusion(bf16[2,1024,768]{2,1,0:T(8,128)(2,1)S(1)} %bitcast.40, bf16[2,1024,3072]{2,1,0:T(8,128)(2,1)} %fusion.9, bf16[768,3072]{1,0:T(8,128)(2,1)S(1)} %copy-done.3), kind=kOutput, calls=%fused_computation.40 | convolution fusion | flops 9668395008 | bytes 23592960 | tf_op jit(solution)/shard_map/mtf,df->mtd/dot_general | solution.py:22
  72.1 0.0 copy-start.8
  72.1 22.0 %fusion.33 = bf16[2,3072,768]{2,1,0:T(8,128)(2,1)} fusion(bf16[2,1024,768]{2,1,0:T(8,128)(2,1)S(1)} %add_convert_fusion, bf16[2,1024,3072]{2,1,0:T(8,128)(2,1)} %bitcast.36), kind=kOutput, calls=%fused_computation.39 | convolution fusion | flops 9731309568 | bytes 25165824 | tf_op jit(solution)/shard_map/mtf,mtd->mfd/dot_general | solution.py:26
  94.1 0.0 copy-done.8
  94.1 0.0 copy-done
  94.1 36.5 %convert_bitcast_fusion = bf16[2,768,3072]{1,2,0:T(8,128)(2,1)} fusion(bf16[2,1024,768]{2,1,0:T(8,128)(2,1)S(1)} %bitcast.33, bf16[2,1024,3072]{2,1,0:T(8,128)(2,1)} %bitcast.37, bf16[2,1024,768]{2,1,0:T(8,128)(2,1)} %copy-done.8, bf16[3072,768]{1,0:T(8,128)(2,1)} %param.14), kind=kOutput, calls=%fused_computation.35 | convolution fusion | flops 19457900544 | bytes 33030144 | tf_op jit(solution)/shard_map/mtd,mtf->mdf/dot_general | solution.py:29
  130.6 0.0 copy-start.5
  130.6 12.9 %copy.24 = bf16[2,768,3072]{2,1,0:T(8,128)(2,1)} copy(bf16[2,768,3072]{1,2,0:T(8,128)(2,1)} %convert_bitcast_fusion) | data formatting | bytes 18874368 | tf_op jit(solution)/shard_map/convert_element_type | solution.py:29
  143.5 16.0 %concatenate.15 = bf16[2,1,2359296]{2,0,1:T(2,128)(2,1)} reshape(bf16[2,768,3072]{2,1,0:T(8,128)(2,1)} %copy.24) | data formatting | bytes 18874368 | tf_op jit(solution)/shard_map/concatenate | solution.py:31
  159.5 11.2 concatenate.14
  170.7 0.0 copy-done.5
  170.8 15.5 %convert_bitcast_fusion.1 = bf16[2,768,3072]{1,2,0:T(8,128)(2,1)} fusion(bf16[2,1024,3072]{2,1,0:T(8,128)(2,1)} %fusion.9, bf16[2,1024,768]{2,1,0:T(8,128)(2,1)S(1)} %bitcast.41), kind=kOutput, calls=%fused_computation.36 | convolution fusion | flops 9668395008 | bytes 25165824 | tf_op jit(solution)/shard_map/mtd,mtf->mdf/dot_general | solution.py:21
  186.3 12.9 %copy.21 = bf16[2,768,3072]{2,1,0:T(8,128)(2,1)} copy(bf16[2,768,3072]{1,2,0:T(8,128)(2,1)} %convert_bitcast_fusion.1) | data formatting | bytes 18874368 | tf_op jit(solution)/shard_map/convert_element_type | solution.py:21
  199.2 16.0 %concatenate.13 = bf16[2,1,2359296]{2,0,1:T(2,128)(2,1)} reshape(bf16[2,768,3072]{2,1,0:T(8,128)(2,1)} %copy.21) | data formatting | bytes 18874368 | tf_op jit(solution)/shard_map/concatenate | solution.py:31
  215.2 11.3 concatenate.12
  226.5 73.1 %pad_maximum_fusion = bf16[2,4,2359296]{2,0,1:T(2,128)(2,1)} fusion(bf16[2,1,2359296]{2,0,1:T(2,128)(2,1)} %concatenate.15, bf16[2,1,2359296]{2,0,1:T(2,128)(2,1)} %concatenate.14, bf16[2,1,2359296]{2,0,1:T(2,128)(2,1)} %concatenate.13, bf16[2,1,2359296]{2,0,1:T(2,128)(2,1)} %concatenate.12), kind=kLoop, calls=%fused_computation.11 | loop fusion | flops 56623104 | bytes 75497472 | tf_op jit(solution)/shard_map/concatenate | solution.py:31
  299.6 428.3 %all_to_all.5 = bf16[2,4,2359296]{2,0,1:T(2,128)(2,1)} all-to-all(bf16[2,4,2359296]{2,0,1:T(2,128)(2,1)} %pad_maximum_fusion), channel_id=1, replica_groups=mesh['dz'=2,'dy'=2,'dx'=4] {'dx'}, dimensions={1} | all-to-all | bytes 75497472 | tf_op jit(solution)/shard_map/all_to_all | solution.py:45
  727.8 0.0 copy-start.7
  727.8 0.0 copy-start.6
  727.8 0.0 copy-start.1
  727.8 103.0 %convert_reduce_fusion = f32[2359296]{0:T(1024)} fusion(bf16[2,4,2359296]{2,0,1:T(2,128)(2,1)} %all_to_all.5), kind=kLoop, calls=%fused_computation | loop fusion | flops 35389440 | bytes 47185920 | tf_op jit(solution)/shard_map/reduce_sum | solution.py:46
  830.8 0.0 all-reduce.5.cloned.1.call-update
  830.8 0.0 all-reduce.7.cloned.1.call-start
  830.9 0.0 copy-done.7
  830.9 0.6 dynamic-slice
  832.1 216.5 %all-reduce.5.cloned.1.call-done = f32[2359296]{0:T(1024)} async-done(((f32[2359296]{0:T(1024)}), f32[2359296]{0:T(1024)}) %all-reduce.5.cloned.1.call-update) | async-done | bytes 9437200
  1048.6 4.1 dynamic-slice.1
  1052.6 0.0 all-reduce.7.cloned.1.call-update
  1052.7 0.0 copy-done.6
  1052.7 0.6 dynamic-slice.2
  1053.9 114.1 %all-reduce.7.cloned.1.call-done = f32[1179648]{0:T(1024)} async-done(((f32[1179648]{0:T(1024)}), f32[1179648]{0:T(1024)}) %all-reduce.7.cloned.1.call-update) | async-done | bytes 4718608
  1168.0 3.2 dynamic-slice.3
  1171.3 0.0 copy-done.1
Async XLA Ops:
  6.5 87.6 %copy-start = (bf16[2048,768]{1,0:T(8,128)(2,1)S(1)}, bf16[2048,768]{1,0:T(8,128)(2,1)}, u32[]{:S(2)}) copy-start(bf16[2048,768]{1,0:T(8,128)(2,1)} %param.8) | copy-start | bytes 9437188
  6.5 1042.0 %all-reduce.5.cloned.1.call-start = ((), (), s32[]{:S(2)}) async-start(), calls=%async_computation.1 | async-start | bytes 18874368
  6.5 23.0 %copy-start.2 = (bf16[3072,768]{1,0:T(8,128)(2,1)S(1)}, bf16[3072,768]{1,0:T(8,128)(2,1)}, u32[]{:S(2)}) copy-start(bf16[3072,768]{1,0:T(8,128)(2,1)} %param.15) | copy-start | bytes 14155780
  29.6 29.5 %copy-start.3 = (bf16[768,3072]{1,0:T(8,128)(2,1)S(1)}, bf16[768,3072]{1,0:T(8,128)(2,1)}, u32[]{:S(2)}) copy-start(bf16[768,3072]{1,0:T(8,128)(2,1)} %param.13) | copy-start | bytes 14155780
  29.6 29.5 %copy-start.4 = (bf16[2048,768]{1,0:T(8,128)(2,1)S(1)}, bf16[2048,768]{1,0:T(8,128)(2,1)}, u32[]{:S(2)}) copy-start(bf16[2048,768]{1,0:T(8,128)(2,1)} %param.12) | copy-start | bytes 9437188
  72.1 22.0 %copy-start.8 = (bf16[2,1024,768]{2,1,0:T(8,128)(2,1)}, bf16[2,1024,768]{2,1,0:T(8,128)(2,1)S(1)}, u32[]{:S(2)}) copy-start(bf16[2,1024,768]{2,1,0:T(8,128)(2,1)S(1)} %add_convert_fusion) | copy-start | bytes 9437188
  130.6 40.1 %copy-start.5 = (bf16[2048,768]{1,0:T(8,128)(2,1)S(1)}, bf16[2048,768]{1,0:T(8,128)(2,1)}, u32[]{:S(2)}) copy-start(bf16[2048,768]{1,0:T(8,128)(2,1)} %param.10) | copy-start | bytes 9437188
  727.8 103.0 %copy-start.7 = (u32[16]{0:T(128)S(1)}, u32[16]{0:T(128)}, u32[]{:S(2)}) copy-start(u32[16]{0:T(128)} %constant.17) | copy-start | bytes 196
  727.8 324.8 %copy-start.6 = (u32[16]{0:T(128)S(1)}, u32[16]{0:T(128)}, u32[]{:S(2)}) copy-start(u32[16]{0:T(128)} %constant.21) | copy-start | bytes 196
  727.8 443.4 %copy-start.1 = (bf16[2048,768]{1,0:T(8,128)(2,1)S(1)}, bf16[2048,768]{1,0:T(8,128)(2,1)}, u32[]{:S(2)}) copy-start(bf16[2048,768]{1,0:T(8,128)(2,1)} %param.8) | copy-start | bytes 9437188
  830.8 337.2 %all-reduce.7.cloned.1.call-start = ((), (), s32[]{:S(2)}) async-start(), calls=%async_computation.2 | async-start | bytes 9437184
Sparse Core Ops, SparseCore 0:
  830.9 217.5 all-reduce.4
  1052.8 115.2 all-reduce.6
where the time goes:
time: 1190 us; the launch traced here: 1180 us
  blocking collectives  428 us (36%)
  waiting for transfers between devices  331 us (28%)
  other arithmetic  176 us (15%)
  matrix products  140 us (12%)
  local copies, waits for them, and re-layouts  88.8 us (7%)
  between operations  15.2 us (1%)
    all_to_all x1, blocking collectives, per_device(): incoming = lax.all_to_all(outgoing, 'dx', 1, 1, tiled=True)  428 us
    unnamed x4, waiting for transfers between devices  331 us
    reduce_sum x1, other arithmetic, per_device(): part_sum = jnp.sum(incoming, axis=(0, 1), dtype=jnp.float32)  103 us
    concatenate x1, other arithmetic, local_grads(): jnp.concatenate([grad_piece.reshape(batch_count, -1) for grad_piece in (g...  73.1 us
    concatenate x4, local copies, waits for them, and re-layouts, local_grads(): jnp.concatenate([grad_piece.reshape(batch_count, -1) for grad_piece in (g...  54.4 us
    dot_general x1, matrix products, local_grads(): jnp.einsum('mtd,mtf->mdf', act_one, d_pre_one, preferred_element_type=jnp...  36.5 us
    dot_general x1, matrix products, local_grads(): jnp.einsum('mtd,fd->mtf', grad_out, w_out_two, preferred_element_type=jnp...  29.5 us
  transfers between devices with their start and end apart: 2, of which 2 were waited for; matrix products, arithmetic and copies ran while one was open for 0% of the time, Pallas kernels for 0%

commit v1 on v0

v1 whole, which is shorter than its diff:
```python
import math

import jax
import jax.numpy as jnp
from jax import lax
from jax.experimental import pallas as pl
from jax.experimental.pallas import tpu as pltpu
from jax.sharding import PartitionSpec as P

MESH = pl.DeviceIdType.MESH
D = 768
FF = 3072
ROWS = 2048
MICRO = 1024
UNITS = 6
WIDE = 512
STEPS = 2 * UNITS
SLOTS = 6
LAG1, LAG2, LAG3 = 2, 4, 6
N_SUM = LAG3 + 1
PARTS = (('yzx', 256), ('zyx', 256), ('xyz', 128), ('xzy', 128))
ROOT = math.sqrt(2.0 / math.pi)
CUBE = 0.044715


def gelu_pair(val):
    sq = val * val
    tan = jnp.tanh(val * (sq * (ROOT * CUBE) + ROOT))
    cdf = 0.5 * tan + 0.5
    bump = val * (cdf * (1.0 - cdf))
    return val * cdf, cdf + bump * (sq * (6.0 * ROOT * CUBE) + 2.0 * ROOT)


def part_layout():
    start = 0
    table = []
    for order, rows in PARTS:
        table.append((order, start, rows))
        start += rows
    return table


def landing_dims(order, stage):
    done = order[:stage + 1]
    return (1 if 'y' in done else 2), (1 if 'z' in done else 2)


def kernel(a1_hbm, z1_hbm, a2_hbm, z2_hbm, g_hbm, wi_hbm, wo1_hbm, wo2_hbm, out_ref,
           dy_v, x_v, acc_v, z_v, h_v, dz_v, wo_v, wi_v, big, drecv, *rest):
    landings = rest[:12]
    isem, fsem, dsend_sem, drecv_sem, send_sem, recv_sem = rest[12:]
    f32, bf16 = jnp.float32, jnp.bfloat16
    dx, y, z = lax.axis_index('dx'), lax.axis_index('dy'), lax.axis_index('dz')
    x, core = dx // 2, dx % 2
    peers = {'x': {'dx': (dx + 2) % 4}, 'y': {'dy': 1 - y}, 'z': {'dz': 1 - z}, 'c': {'dx': dx + 1 - 2 * core}}

    barrier = pltpu.get_barrier_semaphore()
    for name in 'xyzc':
        pl.semaphore_signal(barrier, inc=1, device_id=peers[name], device_id_type=MESH)

    load_g = pltpu.make_async_copy(g_hbm, dy_v, isem.at[0])
    load_2 = pltpu.make_async_copy(a2_hbm, x_v.at[0], isem.at[1])
    load_1 = pltpu.make_async_copy(a1_hbm, x_v.at[1], isem.at[2])

    def fetch(unit, slot, z_hbm, wo_hbm, with_wi):
        copies = []
        for quarter in range(4):
            cols = pl.ds(pl.multiple_of(quarter * 768 + unit * 128, 128), 128)
            put = pl.ds(quarter * 128, 128)
            copies.append(pltpu.make_async_copy(z_hbm.at[:, cols], z_v.at[slot, :, put], fsem.at[slot, quarter]))
            copies.append(pltpu.make_async_copy(wo_hbm.at[cols, :], wo_v.at[slot, put, :], fsem.at[slot, 4 + quarter]))
            if with_wi:
                copies.append(pltpu.make_async_copy(wi_hbm.at[:, cols], wi_v.at[slot, :, put], fsem.at[slot, 8 + quarter]))
        return copies

    def fetch_start(step):
        @pl.when(step < UNITS)
        def _():
            for cp in fetch(step, step % 2, z2_hbm, wo2_hbm, True):
                cp.start()

        @pl.when((step >= UNITS) & (step < STEPS))
        def _():
            for cp in fetch(step - UNITS, step % 2, z1_hbm, wo1_hbm, False):
                cp.start()

    def fetch_wait(step):
        @pl.when(step < UNITS)
        def _():
            for cp in fetch(step, step % 2, z2_hbm, wo2_hbm, True):
                cp.wait()

        @pl.when((step >= UNITS) & (step < STEPS))
        def _():
            for cp in fetch(step - UNITS, step % 2, z1_hbm, wo1_hbm, False):
                cp.wait()

    load_g.start()
    fetch_start(0)
    load_2.start()
    load_1.start()
    pl.semaphore_wait(barrier, 4)
    load_g.wait()

    def d2d_copy(unit):
        return pltpu.make_async_remote_copy(src_ref=big.at[N_SUM], dst_ref=drecv.at[unit % 2], send_sem=dsend_sem.at[0],
                                            recv_sem=drecv_sem.at[unit % 2], device_id=peers['c'], device_id_type=MESH)

    layout = part_layout()

    def views(order, stage, start, rows, unit):
        slot = unit % N_SUM
        done, axis = order[:stage], order[stage]
        keep_y = pl.ds(y, 1) if ('y' in done or axis == 'y') else pl.ds(0, 2)
        keep_z = pl.ds(z, 1) if ('z' in done or axis == 'z') else pl.ds(0, 2)
        away_y = pl.ds(1 - y, 1) if axis == 'y' else keep_y
        away_z = pl.ds(1 - z, 1) if axis == 'z' else keep_z
        away = big.at[slot, away_y, away_z, pl.ds(start, rows), :]
        return away, keep_y, keep_z

    def stage_copy(idx, stage, unit):
        order, start, rows = layout[idx]
        away, _, _ = views(order, stage, start, rows, unit)
        slot = unit % SLOTS
        return pltpu.make_async_remote_copy(src_ref=away, dst_ref=landings[idx * 3 + stage].at[slot],
                                            send_sem=send_sem.at[idx * 3 + stage, slot], recv_sem=recv_sem.at[idx * 3 + stage, slot],
                                            device_id=peers[order[stage]], device_id_type=MESH)

    def stage_roles(idx, stage, unit):
        order = layout[idx][0]
        owner = x == unit // UNITS
        if order[stage] == 'x':
            return x != unit // UNITS, owner
        if 'x' in order[:stage]:
            return owner, owner
        return None, None

    def guarded(cond, body):
        if cond is None:
            body()
        else:
            pl.when(cond)(body)

    def stage_send(idx, stage, unit):
        send_if, _ = stage_roles(idx, stage, unit)
        guarded(send_if, lambda: stage_copy(idx, stage, unit).start())

    def stage_take(idx, stage, unit):
        order, start, rows = layout[idx]
        send_if, recv_if = stage_roles(idx, stage, unit)
        ny, nz = landing_dims(order, stage)
        sum_slot, slot = unit % N_SUM, unit % SLOTS
        land = landings[idx * 3 + stage]
        done = order[:stage + 1]

        def take():
            stage_copy(idx, stage, unit).wait_recv()
            for iy in range(ny):
                for iz in range(nz):
                    at_y = y if 'y' in done else iy
                    at_z = z if 'z' in done else iz

                    def chunk(k, carry):
                        offset = pl.multiple_of(k * 64, 64)
                        here = (sum_slot, at_y, at_z, pl.ds(start + offset, 64), slice(None))
                        big[here] = big[here] + land[slot, iy, iz, pl.ds(offset, 64), :]
                        return carry

                    lax.fori_loop(0, rows // 64, chunk, 0)

        guarded(send_if, lambda: stage_copy(idx, stage, unit).wait_send())
        guarded(recv_if, take)

    def chip_sum(unit):
        cp = d2d_copy(unit)
        cp.wait()
        sum_slot = unit % N_SUM
        for iy in range(2):
            for iz in range(2):
                def chunk(k, carry):
                    here = pl.ds(pl.multiple_of(k * 64, 64), 64)
                    big[sum_slot, iy, iz, here, :] = big[sum_slot, iy, iz, here, :] + drecv[unit % 2, iy, iz, here, :]
                    return carry

                lax.fori_loop(0, 768 // 64, chunk, 0)

    def finish(unit):
        sum_slot, pos = unit % N_SUM, unit % UNITS

        @pl.when((x == unit // UNITS) & (core == 0))
        def _():
            for j in range(6):
                out_ref[pl.ds(768 * pos + j, 128, stride=6), :] = big[sum_slot, y, z, pl.ds(128 * j, 128), :]

        @pl.when((x == unit // UNITS) & (core == 1))
        def _():
            for q in range(4):
                out_ref[pl.ds(6 * q + pos, 192, stride=24), :] = big[sum_slot, y, z, pl.ds(192 * q, 192), :]

    def step_body(step, carry):
        slot = step % 2
        phase = jnp.where(step >= UNITS, 1, 0)

        @pl.when(step < STEPS)
        def _():
            fetch_wait(step)
            fetch_start(step + 1)

            def tile(t, c):
                rows = pl.ds(pl.multiple_of(t * 256, 256), 256)
                hid, slope = gelu_pair(z_v[slot, rows, :].astype(f32))
                h_v[rows, :] = hid.astype(bf16)
                dh = lax.dot_general(dy_v[rows, :], wo_v[slot], (((1,), (1,)), ((), ())), preferred_element_type=f32)
                dz_v[rows, :] = (dh * slope).astype(bf16)
                return c

            lax.fori_loop(0, ROWS // 256, tile, 0)

        @pl.when((step >= 1) & (step <= STEPS))
        def _():
            unit = step - 1
            chip_sum(unit)
            for idx in range(4):
                stage_send(idx, 0, unit)

        for lag, stage in ((LAG1, 0), (LAG2, 1), (LAG3, 2)):
            unit = step - 1 - lag

            @pl.when((unit >= 0) & (unit < STEPS))
            def _(unit=unit, stage=stage):
                for idx in range(4):
                    stage_take(idx, stage, unit)
                    if stage < 2:
                        stage_send(idx, stage + 1, unit)
                if stage == 2:
                    finish(unit)

        @pl.when(step < STEPS)
        def _():
            own = step % N_SUM
            slot_a = jnp.where(core == 0, own, N_SUM)
            slot_b = jnp.where(core == 0, N_SUM, own)

            def grad_a(nb, c):
                cols = pl.ds(pl.multiple_of(nb * 256, 256), 256)
                total = None
                for m in range(2):
                    rows = pl.ds(m * MICRO, MICRO)
                    got = lax.dot_general(h_v[rows, :], dy_v[rows, cols], (((0,), (0,)), ((), ())), preferred_element_type=f32)
                    got = got.astype(bf16).astype(f32)
                    total = got if total is None else total + got
                for q in range(4):
                    for j in range(2):
                        big[slot_a, q // 2, q % 2, pl.ds(pl.multiple_of((2 * nb + j) * 128, 128), 128), :] = total[128 * q:128 * q + 128, 128 * j:128 * j + 128]
                return c

            lax.fori_loop(0, 3, grad_a, 0)
            pl.when(core == 1)(lambda: d2d_copy(step).start())

            @pl.when(step == 0)
            def _():
                load_2.wait()

            @pl.when(step == UNITS)
            def _():
                load_1.wait()

            def grad_b(nb, c):
                cols = pl.ds(pl.multiple_of(nb * 256, 256), 256)
                total = None
                for m in range(2):
                    rows = pl.ds(m * MICRO, MICRO)
                    got = lax.dot_general(x_v[phase, rows, :], dz_v[rows, cols], (((0,), (0,)), ((), ())), preferred_element_type=f32)
                    got = got.astype(bf16).astype(f32)
                    total = got if total is None else total + got
                for q in range(4):
                    for j in range(2):
                        big[slot_b, q // 2, q % 2, pl.ds(pl.multiple_of((2 * nb + j) * 192, 64), 192), :] = total[192 * q:192 * q + 192, 128 * j:128 * j + 128]
                return c

            lax.fori_loop(0, 2, grad_b, 0)
            pl.when(core == 0)(lambda: d2d_copy(step).start())

        @pl.when(step < UNITS)
        def _():
            def back(t, c):
                rows = pl.ds(pl.multiple_of(t * 512, 512), 512)
                add = lax.dot_general(dz_v[rows, :], wi_v[slot], (((1,), (1,)), ((), ())), preferred_element_type=f32)

                @pl.when(step == 0)
                def _():
                    acc_v[rows, :] = add

                @pl.when(step > 0)
                def _():
                    acc_v[rows, :] = acc_v[rows, :] + add
                return c

            lax.fori_loop(0, ROWS // 512, back, 0)

        @pl.when(step == UNITS - 1)
        def _():
            def close(t, c):
                rows = pl.ds(pl.multiple_of(t * 32, 32), 32)
                dy_v[rows, :] = (dy_v[rows, :].astype(f32) + acc_v[rows, :]).astype(bf16)
                return c

            lax.fori_loop(0, ROWS // 32, close, 0)

        return carry

    lax.fori_loop(0, STEPS + 1 + LAG3, step_body, 0)


def solution(mesh):
    row_spec = P(('dz', 'dy', 'dx'), None)
    full_spec = P(None, None)

    def per_device(*arrays):
        f32, bf16 = jnp.float32, jnp.bfloat16
        landings = []
        for order, rows in PARTS:
            for stage in range(3):
                ny, nz = landing_dims(order, stage)
                landings.append(pltpu.VMEM((SLOTS, ny, nz, rows, 128), f32))
        out = pl.pallas_call(
            kernel,
            out_shape=jax.ShapeDtypeStruct((4608, 128), f32),
            in_specs=[pl.BlockSpec(memory_space=pl.ANY)] * 8,
            out_specs=pl.BlockSpec(memory_space=pltpu.VMEM),
            scratch_shapes=[
                pltpu.VMEM((ROWS, D), bf16),
                pltpu.VMEM((2, ROWS, D), bf16),
                pltpu.VMEM((ROWS, D), f32),
                pltpu.VMEM((2, ROWS, WIDE), bf16),
                pltpu.VMEM((ROWS, WIDE), bf16),
                pltpu.VMEM((ROWS, WIDE), bf16),
                pltpu.VMEM((2, WIDE, D), bf16),
                pltpu.VMEM((2, D, WIDE), bf16),
                pltpu.VMEM((N_SUM + 1, 2, 2, 768, 128), f32),
                pltpu.VMEM((2, 2, 2, 768, 128), f32),
                *landings,
                pltpu.SemaphoreType.DMA((3,)),
                pltpu.SemaphoreType.DMA((2, 12)),
                pltpu.SemaphoreType.DMA((1,)),
                pltpu.SemaphoreType.DMA((2,)),
                pltpu.SemaphoreType.DMA((12, SLOTS)),
                pltpu.SemaphoreType.DMA((12, SLOTS)),
            ],
            compiler_params=pltpu.CompilerParams(collective_id=0, has_side_effects=True, vmem_limit_bytes=67043328),
        )(*arrays)
        return out.reshape(-1)

    return jax.shard_map(per_device, mesh=mesh, in_specs=(row_spec,) * 5 + (full_spec,) * 3, out_specs=P(('dx', 'dy', 'dz')), check_vma=False)
```

time: 1190 us -> 203 us (0.17)
  blocking collectives: 428 us -> 0 us
  waiting for transfers between devices: 331 us -> 0 us
  Pallas kernels: 0 us -> 199 us
  other arithmetic: 176 us -> 0 us
  matrix products: 140 us -> 0 us
  local copies, waits for them, and re-layouts: 88.8 us -> 3.22 us
  between operations: 15.2 us -> 0.01 us
    all_to_all x1 -> x0, blocking collectives: 428 us -> none  [per_device(): incoming = lax.all_to_all(outgoing, 'dx', 1, 1, tiled=True)]
    unnamed x4 -> x0, waiting for transfers between devices: 331 us -> none
    pallas_call x0 -> x1, Pallas kernels: none -> 199 us  [per_device(): pl.pallas_call(kernel, out_shape=jax.ShapeDtypeStruct((4608, 128), f32),...]
    dot_general x6 -> x0, matrix products: 140 us -> none  [the longest x1 36.5 us: local_grads(): jnp.einsum('mtd,mtf->mdf', act_one, d_pre_one, preferred_element_type=jnp...]
    reduce_sum x1 -> x0, other arithmetic: 103 us -> none  [per_device(): part_sum = jnp.sum(incoming, axis=(0, 1), dtype=jnp.float32)]
    concatenate x1 -> x0, other arithmetic: 73.1 us -> none  [local_grads(): jnp.concatenate([grad_piece.reshape(batch_count, -1) for grad_piece in (g...]
    concatenate x4 -> x0, local copies, waits for them, and re-layouts: 54.4 us -> none  [local_grads(): jnp.concatenate([grad_piece.reshape(batch_count, -1) for grad_piece in (g...]
    convert_element_type x2 -> x0, local copies, waits for them, and re-layouts: 25.9 us -> none  [the longest x1 12.9 us: local_grads(): jnp.einsum('mtd,mtf->mdf', act_two, d_pre_two, preferred_element_type=jnp...]
  transfers between devices with their start and end apart: 2 -> 0, of which waited for: 2 -> 0; matrix products, arithmetic and copies ran while one was open for 0% -> 0% of each run, Pallas kernels for 0% -> 0%
where the time goes in v1:
time: 203 us; the launch traced here: 202 us
  Pallas kernels  199 us (98%)
  local copies, waits for them, and re-layouts  3.22 us (2%)
    pallas_call x1, Pallas kernels, per_device(): pl.pallas_call(kernel, out_shape=jax.ShapeDtypeStruct((4608, 128), f32),...  199 us

profile of v1, /device:TPU:0, one launch (start us, length us, event | category | flops | bytes accessed | tf_op | source)
XLA Modules:
  0.0 202.3 jit_solution(6351027340487896711)
XLA Ops:
  0.0 199.1 %shard_map.82 = f32[4608,128]{1,0:T(8,128)} custom-call(bf16[2048,768]{1,0:T(8,128)(2,1)} %a1_hbm.1, bf16[2048,3072]{1,0:T(8,128)(2,1)} %z1_hbm.1, bf16[2048,768]{1,0:T(8,128)(2,1)} %a2_hbm.1, bf16[2048,3072]{1,0:T(8,128)(2,1)} %z2_hbm.1, bf16[2048,768]{1,0:T(8,128)(2,1)} %g_hbm.1, bf16[768,3072]{1,0:T(8,128)(2,1)} %wi_hbm.1, bf16[3072,768]{1,0:T(8,128)(2,1)} %wo1_hbm.1, ...), custom_call_target="tpu_custom_call" | custom-call | tf_op jit(solution)/shard_map/pallas_call | solution.py:326
  199.1 3.2 %copy.10 = f32[589824]{0:T(1024)} copy(f32[589824]{0:T(1024)} %bitcast.1) | data formatting | bytes 4718592

commit v2 on v0

v2 whole, which is shorter than its diff:
```python
import math

import jax
import jax.numpy as jnp
from jax import lax
from jax.experimental import pallas as pl
from jax.experimental.pallas import tpu as pltpu
from jax.sharding import PartitionSpec as P

MESH = pl.DeviceIdType.MESH
D = 768
FF = 3072
ROWS = 2048
MICRO = 1024
UNITS = 6
WIDE = 512
STEPS = 2 * UNITS
SLOTS = 6
ORDERS = ('yzx', 'zyx', 'xyz', 'xzy', 'wyzx', 'wzyx')
TAKES = {
    (0, 0): (7, 11, 15, 19, 23, 27, 37, 41, 47, 53, 59, 65),
    (0, 1): (11, 15, 19, 25, 29, 33, 49, 55, 62, 68, 71, 73),
    (0, 2): (19, 23, 33, 41, 45, 47, 49, 58, 62, 68, 72, 75),
    (1, 0): (9, 13, 17, 21, 29, 37, 37, 37, 41, 45, 52, 55),
    (1, 1): (13, 17, 21, 25, 35, 47, 47, 49, 54, 60, 66, 69),
    (1, 2): (17, 21, 25, 29, 43, 58, 58, 66, 69, 71, 73, 74),
    (2, 0): (9, 13, 17, 21, 25, 29),
    (2, 1): (13, 17, 21, 25, 31, 37),
    (2, 2): (17, 21, 25, 31, 37, 49),
    (2, 3): (25, 33, 39, 43, 48, 51),
}
FINISH = (25, 33, 39, 43, 48, 58, 58, 66, 69, 71, 73, 75)
N_SUM = 8
TICKS = 76
ROWS_ONE = (192, 192, 96, 96, 96, 96)
ROWS_TWO = (320, 320, 64, 64, 0, 0)
ROOT = math.sqrt(2.0 / math.pi)
CUBE = 0.044715


def gelu_pair(val):
    sq = val * val
    tan = jnp.tanh(val * (sq * (ROOT * CUBE) + ROOT))
    cdf = 0.5 * tan + 0.5
    bump = val * (cdf * (1.0 - cdf))
    return val * cdf, cdf + bump * (sq * (6.0 * ROOT * CUBE) + 2.0 * ROOT)


def landing_dims(order, stage):
    done = order[:stage + 1]
    return (1 if 'y' in done else 2), (1 if 'z' in done else 2)


def stage_list():
    return [(idx, stage) for idx, order in enumerate(ORDERS) for stage in range(len(order))]


STAGES = stage_list()


def kernel(a1_hbm, z1_hbm, a2_hbm, z2_hbm, g_hbm, wi_hbm, wo1_hbm, wo2_hbm, out_ref,
           dy_v, x_v, acc_v, z_v, hnew_v, h_v, slope_v, dz_v, wo_v, wi_v, big, drecv, *rest):
    landings = dict(zip(STAGES, rest[:len(STAGES)]))
    isem, zsem, osem, wsem, dsend_sem, drecv_sem, send_sem, recv_sem = rest[len(STAGES):]
    f32, bf16 = jnp.float32, jnp.bfloat16
    dx, y, z = lax.axis_index('dx'), lax.axis_index('dy'), lax.axis_index('dz')
    x, core = dx // 2, dx % 2
    peers = {'x': {'dx': (dx + 2) % 4}, 'y': {'dy': 1 - y}, 'z': {'dz': 1 - z}, 'c': {'dx': dx + 1 - 2 * core}}
    peers['w'] = peers['x']

    barrier = pltpu.get_barrier_semaphore()
    for name in 'xyzc':
        pl.semaphore_signal(barrier, inc=1, device_id=peers[name], device_id_type=MESH)

    load_g = pltpu.make_async_copy(g_hbm, dy_v, isem.at[0])
    load_2 = pltpu.make_async_copy(a2_hbm, x_v, isem.at[1])
    load_1 = pltpu.make_async_copy(a1_hbm, x_v, isem.at[2])

    def columns(unit, quarter):
        return pl.ds(pl.multiple_of(quarter * 768 + unit * 128, 128), 128), pl.ds(quarter * 128, 128)

    def z_copies(unit, hbm):
        pairs = [columns(unit, q) for q in range(4)]
        return [pltpu.make_async_copy(hbm.at[:, get], z_v.at[:, put], zsem.at[q]) for q, (get, put) in enumerate(pairs)]

    def wo_copies(unit, hbm):
        pairs = [columns(unit, q) for q in range(4)]
        return [pltpu.make_async_copy(hbm.at[get, :], wo_v.at[put, :], osem.at[q]) for q, (get, put) in enumerate(pairs)]

    def wi_copies(unit):
        pairs = [columns(unit, q) for q in range(4)]
        return [pltpu.make_async_copy(wi_hbm.at[:, get], wi_v.at[:, put], wsem.at[q]) for q, (get, put) in enumerate(pairs)]

    def by_phase(step, make, action):
        @pl.when(step < UNITS)
        def _():
            for cp in make(step, 0):
                action(cp)

        @pl.when((step >= UNITS) & (step < STEPS))
        def _():
            for cp in make(step - UNITS, 1):
                action(cp)

    def z_make(unit, phase):
        return z_copies(unit, z1_hbm if phase else z2_hbm)

    def wo_make(unit, phase):
        return wo_copies(unit, wo1_hbm if phase else wo2_hbm)

    def start(cp):
        cp.start()

    def wait(cp):
        cp.wait()

    for cp in z_copies(0, z2_hbm):
        cp.start()
    for cp in wo_copies(0, wo2_hbm):
        cp.start()
    load_g.start()
    load_2.start()
    for cp in wi_copies(0):
        cp.start()

    def gelu_rows(start, count):
        for k in range(count // 32):
            rows = pl.ds(pl.multiple_of(start + k * 32, 32), 32)
            hid, slope = gelu_pair(z_v[rows, :].astype(f32))
            hnew_v[rows, :] = hid.astype(bf16)
            slope_v[rows, :] = slope

    for cp in z_copies(0, z2_hbm):
        cp.wait()

    def first_gelu(t, c):
        gelu_rows(t * 128, 128)
        return c

    lax.fori_loop(0, ROWS // 128, first_gelu, 0)
    for cp in z_copies(1, z2_hbm):
        cp.start()
    load_g.wait()
    pl.semaphore_wait(barrier, 4)

    def d2d_copy(unit):
        return pltpu.make_async_remote_copy(src_ref=big.at[N_SUM], dst_ref=drecv.at[unit % 2], send_sem=dsend_sem.at[0],
                                            recv_sem=drecv_sem.at[unit % 2], device_id=peers['c'], device_id_type=MESH)

    def placed(phase):
        sizes = (ROWS_ONE, ROWS_TWO)[phase]
        starts = [sum(sizes[:k]) for k in range(len(sizes))]
        return list(zip(starts, sizes))

    def stage_copy(idx, stage, unit, phase):
        order = ORDERS[idx]
        first, rows = placed(phase)[idx]
        done, axis = order[:stage], order[stage]
        at_y = pl.ds(1 - y, 1) if axis == 'y' else pl.ds(y, 1) if 'y' in done else pl.ds(0, 2)
        at_z = pl.ds(1 - z, 1) if axis == 'z' else pl.ds(z, 1) if 'z' in done else pl.ds(0, 2)
        slot, sem = unit % SLOTS, STAGES.index((idx, stage))
        return pltpu.make_async_remote_copy(src_ref=big.at[unit % N_SUM, at_y, at_z, pl.ds(first, rows), :],
                                            dst_ref=landings[idx, stage].at[slot, :, :, pl.ds(0, rows), :],
                                            send_sem=send_sem.at[sem, slot], recv_sem=recv_sem.at[sem, slot],
                                            device_id=peers[axis], device_id_type=MESH)

    def roles(idx, stage, phase):
        order = ORDERS[idx]
        if order[stage] == 'w':
            return x == phase, x != phase
        if order[stage] == 'x':
            return x != phase, x == phase
        done = order[:stage]
        if 'x' in done:
            return x == phase, x == phase
        if 'w' in done:
            return x != phase, x != phase
        return None, None

    def guarded(cond, body):
        if cond is None:
            body()
        else:
            pl.when(cond)(body)

    def stage_send(idx, stage, unit, phase):
        guarded(roles(idx, stage, phase)[0], lambda: stage_copy(idx, stage, unit, phase).start())

    def stage_take(idx, stage, unit, phase):
        order = ORDERS[idx]
        first, rows = placed(phase)[idx]
        send_if, recv_if = roles(idx, stage, phase)
        ny, nz = landing_dims(order, stage)
        land, done = landings[idx, stage], order[:stage + 1]
        back = order[0] == 'w' and order[stage] == 'x'
        size = max(n for n in (96, 80, 64, 48, 32) if rows % n == 0)

        def take():
            stage_copy(idx, stage, unit, phase).wait_recv()
            for iy in range(ny):
                for iz in range(nz):
                    at_y = y if 'y' in done else iy
                    at_z = z if 'z' in done else iz

                    def chunk(k, carry):
                        offset = pl.multiple_of(k * size, 16)
                        here = (unit % N_SUM, at_y, at_z, pl.ds(first + offset, size), slice(None))
                        got = land[unit % SLOTS, iy, iz, pl.ds(offset, size), :]
                        big[here] = got if back else big[here] + got
                        return carry

                    lax.fori_loop(0, rows // size, chunk, 0)

        guarded(send_if, lambda: stage_copy(idx, stage, unit, phase).wait_send())
        guarded(recv_if, take)

    def part_list(phase):
        return [idx for idx in range(len(ORDERS)) if placed(phase)[idx][1]]

    def chip_sum(unit):
        d2d_copy(unit).wait()
        for iy in range(2):
            for iz in range(2):
                def chunk(k, carry):
                    here = pl.ds(pl.multiple_of(k * 128, 128), 128)
                    big[unit % N_SUM, iy, iz, here, :] = big[unit % N_SUM, iy, iz, here, :] + drecv[unit % 2, iy, iz, here, :]
                    return carry

                lax.fori_loop(0, 768 // 128, chunk, 0)
        for phase in range(2):
            @pl.when(unit // UNITS == phase)
            def _(phase=phase):
                for idx in part_list(phase):
                    stage_send(idx, 0, unit, phase)

    def finish(unit):
        sum_slot, pos = unit % N_SUM, unit % UNITS

        @pl.when((x == unit // UNITS) & (core == 0))
        def _():
            for j in range(6):
                out_ref[pl.ds(768 * pos + j, 128, stride=6), :] = big[sum_slot, y, z, pl.ds(128 * j, 128), :]

        @pl.when((x == unit // UNITS) & (core == 1))
        def _():
            for q in range(4):
                out_ref[pl.ds(6 * q + pos, 192, stride=24), :] = big[sum_slot, y, z, pl.ds(192 * q, 192), :]

    def reached(tick, row):
        total = jnp.int32(0)
        for value in row:
            total = total + jnp.where(tick >= value, 1, 0)
        return total

    def run_ticks(tick, seen):
        now = []
        for place, (key, row) in enumerate(sorted(TAKES.items())):
            group, stage = key
            count = reached(tick, row)

            def one(unit, carry):
                for phase in range(2):
                    members = [i for i in (2 * group, 2 * group + 1) if placed(phase)[i][1]]
                    if not members:
                        continue

                    @pl.when(unit // UNITS == phase)
                    def _(phase=phase, members=members):
                        for idx in members:
                            stage_take(idx, stage, unit, phase)
                            if stage + 1 < len(ORDERS[idx]):
                                stage_send(idx, stage + 1, unit, phase)
                return carry

            lax.fori_loop(seen[place], count, one, 0)
            now.append(count)
        count = reached(tick, FINISH)

        def last(unit, carry):
            finish(unit)
            return carry

        lax.fori_loop(seen[-1], count, last, 0)
        now.append(count)
        return tuple(now)

    def body(tick, seen):
        step, part = tick // 4, tick % 4
        live = step < STEPS

        @pl.when(live & (part == 0))
        def _():
            by_phase(step, wo_make, wait)

            def tile(t, c):
                rows = pl.ds(pl.multiple_of(t * 256, 256), 256)
                h_v[rows, :] = hnew_v[rows, :]
                dh = lax.dot_general(dy_v[rows, :], wo_v[...], (((1,), (1,)), ((), ())), preferred_element_type=f32)
                dz_v[rows, :] = (dh * slope_v[rows, :]).astype(bf16)
                return c

            lax.fori_loop(0, ROWS // 256, tile, 0)
            by_phase(step + 1, wo_make, start)
            by_phase(step + 1, z_make, wait)

        @pl.when(live & ((part == 1) | (part == 2)))
        def _():
            own = step % N_SUM
            is_a = (part == 1) == (core == 1)
            slot_a = jnp.where(core == 0, own, N_SUM)
            slot_b = jnp.where(core == 0, N_SUM, own)

            @pl.when(is_a)
            def _():
                def grad_a(nb, c):
                    cols = pl.ds(pl.multiple_of(nb * 256, 256), 256)
                    gelu_rows(nb * 384, 384)
                    total = None
                    for m in range(2):
                        rows = pl.ds(m * MICRO, MICRO)
                        got = lax.dot_general(h_v[rows, :], dy_v[rows, cols], (((0,), (0,)), ((), ())), preferred_element_type=f32)
                        got = got.astype(bf16).astype(f32)
                        total = got if total is None else total + got
                    for q in range(4):
                        for j in range(2):
                            here = pl.ds(pl.multiple_of((2 * nb + j) * 128, 128), 128)
                            big[slot_a, q // 2, q % 2, here, :] = total[128 * q:128 * q + 128, 128 * j:128 * j + 128]
                    return c

                lax.fori_loop(0, 3, grad_a, 0)

            @pl.when(jnp.logical_not(is_a))
            def _():
                @pl.when(step == 0)
                def _():
                    load_2.wait()

                @pl.when(step == UNITS)
                def _():
                    load_1.wait()

                def grad_b(nb, c):
                    cols = pl.ds(pl.multiple_of(nb * 256, 256), 256)
                    gelu_rows(1152 + nb * 448, 448)
                    total = None
                    for m in range(2):
                        rows = pl.ds(m * MICRO, MICRO)
                        got = lax.dot_general(x_v[rows, :], dz_v[rows, cols], (((0,), (0,)), ((), ())), preferred_element_type=f32)
                        got = got.astype(bf16).astype(f32)
                        total = got if total is None else total + got
                    for q in range(4):
                        for j in range(2):
                            here = pl.ds(pl.multiple_of((2 * nb + j) * 192, 64), 192)
                            big[slot_b, q // 2, q % 2, here, :] = total[192 * q:192 * q + 192, 128 * j:128 * j + 128]
                    return c

                lax.fori_loop(0, 2, grad_b, 0)

                @pl.when(step == UNITS - 1)
                def _():
                    load_1.start()

            @pl.when(part == 1)
            def _():
                d2d_copy(step).start()

            @pl.when(part == 2)
            def _():
                by_phase(step + 2, z_make, start)

        @pl.when((step < UNITS) & (part == 3))
        def _():
            for cp in wi_copies(step):
                cp.wait()

            def back(t, c):
                rows = pl.ds(pl.multiple_of(t * 512, 512), 512)
                add = lax.dot_general(dz_v[rows, :], wi_v[...], (((1,), (1,)), ((), ())), preferred_element_type=f32)
                acc_v[rows, :] = jnp.where(step == 0, dy_v[rows, :].astype(f32), acc_v[rows, :]) + add
                return c

            lax.fori_loop(0, ROWS // 512, back, 0)

            @pl.when(step < UNITS - 1)
            def _():
                for cp in wi_copies(step + 1):
                    cp.start()

            @pl.when(step == UNITS - 1)
            def _():
                def close(t, c):
                    rows = pl.ds(pl.multiple_of(t * 32, 32), 32)
                    dy_v[rows, :] = acc_v[rows, :].astype(bf16)
                    return c

                lax.fori_loop(0, ROWS // 32, close, 0)

        early = (part == 3) & (step < UNITS)
        late = (part == 0) & (step > UNITS) & (step <= STEPS)

        @pl.when(early | late)
        def _():
            chip_sum(jnp.where(part == 3, step, step - 1))

        return run_ticks(tick, seen)

    lax.fori_loop(0, TICKS, body, (jnp.int32(0),) * (len(TAKES) + 1))


def solution(mesh):
    row_spec = P(('dz', 'dy', 'dx'), None)
    full_spec = P(None, None)

    def per_device(*arrays):
        f32, bf16 = jnp.float32, jnp.bfloat16
        landings = []
        for idx, stage in STAGES:
            ny, nz = landing_dims(ORDERS[idx], stage)
            landings.append(pltpu.VMEM((SLOTS, ny, nz, max(ROWS_ONE[idx], ROWS_TWO[idx]), 128), f32))
        out = pl.pallas_call(
            kernel,
            out_shape=jax.ShapeDtypeStruct((4608, 128), f32),
            in_specs=[pl.BlockSpec(memory_space=pl.ANY)] * 8,
            out_specs=pl.BlockSpec(memory_space=pltpu.VMEM),
            scratch_shapes=[
                pltpu.VMEM((ROWS, D), bf16),
                pltpu.VMEM((ROWS, D), bf16),
                pltpu.VMEM((ROWS, D), f32),
                pltpu.VMEM((ROWS, WIDE), bf16),
                pltpu.VMEM((ROWS, WIDE), bf16),
                pltpu.VMEM((ROWS, WIDE), bf16),
                pltpu.VMEM((ROWS, WIDE), f32),
                pltpu.VMEM((ROWS, WIDE), bf16),
                pltpu.VMEM((WIDE, D), bf16),
                pltpu.VMEM((D, WIDE), bf16),
                pltpu.VMEM((N_SUM + 1, 2, 2, 768, 128), f32),
                pltpu.VMEM((2, 2, 2, 768, 128), f32),
                *landings,
                pltpu.SemaphoreType.DMA((3,)),
                pltpu.SemaphoreType.DMA((4,)),
                pltpu.SemaphoreType.DMA((4,)),
                pltpu.SemaphoreType.DMA((4,)),
                pltpu.SemaphoreType.DMA((1,)),
                pltpu.SemaphoreType.DMA((2,)),
                pltpu.SemaphoreType.DMA((len(STAGES), SLOTS)),
                pltpu.SemaphoreType.DMA((len(STAGES), SLOTS)),
            ],
            compiler_params=pltpu.CompilerParams(collective_id=0, has_side_effects=True, vmem_limit_bytes=67043328),
        )(*arrays)
        return out.reshape(-1)

    return jax.shard_map(per_device, mesh=mesh, in_specs=(row_spec,) * 5 + (full_spec,) * 3, out_specs=P(('dx', 'dy', 'dz')), check_vma=False)
```

time: 1190 us -> 202 us (0.17)
  blocking collectives: 428 us -> 0 us
  waiting for transfers between devices: 331 us -> 0 us
  Pallas kernels: 0 us -> 199 us
  other arithmetic: 176 us -> 0 us
  matrix products: 140 us -> 0 us
  local copies, waits for them, and re-layouts: 88.8 us -> 3.22 us
  between operations: 15.2 us -> 0.01 us
    all_to_all x1 -> x0, blocking collectives: 428 us -> none  [per_device(): incoming = lax.all_to_all(outgoing, 'dx', 1, 1, tiled=True)]
    unnamed x4 -> x0, waiting for transfers between devices: 331 us -> none
    pallas_call x0 -> x1, Pallas kernels: none -> 199 us  [per_device(): pl.pallas_call(kernel, out_shape=jax.ShapeDtypeStruct((4608, 128), f32),...]
    dot_general x6 -> x0, matrix products: 140 us -> none  [the longest x1 36.5 us: local_grads(): jnp.einsum('mtd,mtf->mdf', act_one, d_pre_one, preferred_element_type=jnp...]
    reduce_sum x1 -> x0, other arithmetic: 103 us -> none  [per_device(): part_sum = jnp.sum(incoming, axis=(0, 1), dtype=jnp.float32)]
    concatenate x1 -> x0, other arithmetic: 73.1 us -> none  [local_grads(): jnp.concatenate([grad_piece.reshape(batch_count, -1) for grad_piece in (g...]
    concatenate x4 -> x0, local copies, waits for them, and re-layouts: 54.4 us -> none  [local_grads(): jnp.concatenate([grad_piece.reshape(batch_count, -1) for grad_piece in (g...]
    convert_element_type x2 -> x0, local copies, waits for them, and re-layouts: 25.9 us -> none  [the longest x1 12.9 us: local_grads(): jnp.einsum('mtd,mtf->mdf', act_two, d_pre_two, preferred_element_type=jnp...]
  transfers between devices with their start and end apart: 2 -> 0, of which waited for: 2 -> 0; matrix products, arithmetic and copies ran while one was open for 0% -> 0% of each run, Pallas kernels for 0% -> 0%
where the time goes in v2:
time: 202 us
  Pallas kernels  199 us (99%)
  local copies, waits for them, and re-layouts  3.22 us (2%)
    pallas_call x1, Pallas kernels, per_device(): pl.pallas_call(kernel, out_shape=jax.ShapeDtypeStruct((4608, 128), f32),...  199 us

profile of v2, /device:TPU:0, one launch (start us, length us, event | category | flops | bytes accessed | tf_op | source)
XLA Modules:
  0.0 202.2 jit_solution(15365422429011018958)
XLA Ops:
  0.0 199.0 %shard_map.82 = f32[4608,128]{1,0:T(8,128)} custom-call(bf16[2048,768]{1,0:T(8,128)(2,1)} %a1_hbm.1, bf16[2048,3072]{1,0:T(8,128)(2,1)} %z1_hbm.1, bf16[2048,768]{1,0:T(8,128)(2,1)} %a2_hbm.1, bf16[2048,3072]{1,0:T(8,128)(2,1)} %z2_hbm.1, bf16[2048,768]{1,0:T(8,128)(2,1)} %g_hbm.1, bf16[768,3072]{1,0:T(8,128)(2,1)} %wi_hbm.1, bf16[3072,768]{1,0:T(8,128)(2,1)} %wo1_hbm.1, ...), custom_call_target="tpu_custom_call" | custom-call | tf_op jit(solution)/shard_map/pallas_call | solution.py:420
  199.0 3.2 %copy.10 = f32[589824]{0:T(1024)} copy(f32[589824]{0:T(1024)} %bitcast.1) | data formatting | bytes 4718592

commit v3 on v2

--- a/solution.py
+++ b/solution.py
@@ -16,23 +16,24 @@
 WIDE = 512
 STEPS = 2 * UNITS
 SLOTS = 6
+TILE = 1024
 ORDERS = ('yzx', 'zyx', 'xyz', 'xzy', 'wyzx', 'wzyx')
 TAKES = {
-    (0, 0): (7, 11, 15, 19, 23, 27, 37, 41, 47, 53, 59, 65),
-    (0, 1): (11, 15, 19, 25, 29, 33, 49, 55, 62, 68, 71, 73),
-    (0, 2): (19, 23, 33, 41, 45, 47, 49, 58, 62, 68, 72, 75),
-    (1, 0): (9, 13, 17, 21, 29, 37, 37, 37, 41, 45, 52, 55),
-    (1, 1): (13, 17, 21, 25, 35, 47, 47, 49, 54, 60, 66, 69),
-    (1, 2): (17, 21, 25, 29, 43, 58, 58, 66, 69, 71, 73, 74),
-    (2, 0): (9, 13, 17, 21, 25, 29),
-    (2, 1): (13, 17, 21, 25, 31, 37),
-    (2, 2): (17, 21, 25, 31, 37, 49),
-    (2, 3): (25, 33, 39, 43, 48, 51),
+    (0, 0): (7, 11, 15, 19, 23, 27, 37, 41, 45, 51, 58, 64),
+    (0, 1): (13, 17, 21, 25, 29, 33, 45, 53, 60, 66, 69, 71),
+    (0, 2): (17, 21, 27, 33, 37, 39, 48, 55, 61, 66, 69, 72),
+    (1, 0): (7, 11, 15, 19, 23, 29, 33, 37, 41, 45, 51, 58),
+    (1, 1): (13, 17, 21, 25, 29, 35, 41, 47, 54, 58, 64, 67),
+    (1, 2): (15, 19, 23, 29, 35, 41, 54, 60, 66, 69, 71, 71),
+    (2, 0): (9, 11, 15, 19, 23, 29),
+    (2, 1): (13, 17, 21, 25, 29, 37),
+    (2, 2): (17, 21, 25, 29, 37, 47),
+    (2, 3): (21, 27, 33, 37, 41, 49),
 }
-FINISH = (25, 33, 39, 43, 48, 58, 58, 66, 69, 71, 73, 75)
-N_SUM = 8
-TICKS = 76
-ROWS_ONE = (192, 192, 96, 96, 96, 96)
+FINISH = (21, 27, 33, 37, 41, 49, 54, 60, 66, 69, 71, 72)
+N_SUM = 7
+TICKS = 73
+ROWS_ONE = (224, 224, 64, 64, 96, 96)
 ROWS_TWO = (320, 320, 64, 64, 0, 0)
 ROOT = math.sqrt(2.0 / math.pi)
 CUBE = 0.044715
@@ -193,7 +194,7 @@
         ny, nz = landing_dims(order, stage)
         land, done = landings[idx, stage], order[:stage + 1]
         back = order[0] == 'w' and order[stage] == 'x'
-        size = max(n for n in (96, 80, 64, 48, 32) if rows % n == 0)
+        size = max(n for n in (128, 112, 96, 80, 64, 48, 32) if rows % n == 0)
 
         def take():
             stage_copy(idx, stage, unit, phase).wait_recv()
@@ -293,13 +294,13 @@
             by_phase(step, wo_make, wait)
 
             def tile(t, c):
-                rows = pl.ds(pl.multiple_of(t * 256, 256), 256)
+                rows = pl.ds(pl.multiple_of(t * TILE, TILE), TILE)
                 h_v[rows, :] = hnew_v[rows, :]
                 dh = lax.dot_general(dy_v[rows, :], wo_v[...], (((1,), (1,)), ((), ())), preferred_element_type=f32)
                 dz_v[rows, :] = (dh * slope_v[rows, :]).astype(bf16)
                 return c
 
-            lax.fori_loop(0, ROWS // 256, tile, 0)
+            lax.fori_loop(0, ROWS // TILE, tile, 0)
             by_phase(step + 1, wo_make, start)
             by_phase(step + 1, z_make, wait)
 
@@ -374,12 +375,12 @@
                 cp.wait()
 
             def back(t, c):
-                rows = pl.ds(pl.multiple_of(t * 512, 512), 512)
+                rows = pl.ds(pl.multiple_of(t * TILE, TILE), TILE)
                 add = lax.dot_general(dz_v[rows, :], wi_v[...], (((1,), (1,)), ((), ())), preferred_element_type=f32)
                 acc_v[rows, :] = jnp.where(step == 0, dy_v[rows, :].astype(f32), acc_v[rows, :]) + add
                 return c
 
-            lax.fori_loop(0, ROWS // 512, back, 0)
+            lax.fori_loop(0, ROWS // TILE, back, 0)
 
             @pl.when(step < UNITS - 1)
             def _():

time: 202 us -> 180 us (0.89)
  Pallas kernels: 199 us -> 176 us
    pallas_call x1, Pallas kernels: 199 us -> 176 us  [per_device(): pl.pallas_call(kernel, out_shape=jax.ShapeDtypeStruct((4608, 128), f32),...]
where the time goes in v3:
time: 180 us; the launch traced here: 179 us
  Pallas kernels  176 us (98%)
  local copies, waits for them, and re-layouts  3.22 us (2%)
    pallas_call x1, Pallas kernels, per_device(): pl.pallas_call(kernel, out_shape=jax.ShapeDtypeStruct((4608, 128), f32),...  176 us

profile of v3, /device:TPU:0, one launch (start us, length us, event | category | flops | bytes accessed | tf_op | source)
XLA Modules:
  0.0 179.3 jit_solution(2561151006536802058)
XLA Ops:
  0.0 176.1 %shard_map.82 = f32[4608,128]{1,0:T(8,128)} custom-call(bf16[2048,768]{1,0:T(8,128)(2,1)} %a1_hbm.1, bf16[2048,3072]{1,0:T(8,128)(2,1)} %z1_hbm.1, bf16[2048,768]{1,0:T(8,128)(2,1)} %a2_hbm.1, bf16[2048,3072]{1,0:T(8,128)(2,1)} %z2_hbm.1, bf16[2048,768]{1,0:T(8,128)(2,1)} %g_hbm.1, bf16[768,3072]{1,0:T(8,128)(2,1)} %wi_hbm.1, bf16[3072,768]{1,0:T(8,128)(2,1)} %wo1_hbm.1, ...), custom_call_target="tpu_custom_call" | custom-call | tf_op jit(solution)/shard_map/pallas_call | solution.py:421
  176.1 3.2 %copy.10 = f32[589824]{0:T(1024)} copy(f32[589824]{0:T(1024)} %bitcast.1) | data formatting | bytes 4718592

commit v4 on v3

--- a/solution.py
+++ b/solution.py
@@ -19,18 +19,18 @@
 TILE = 1024
 ORDERS = ('yzx', 'zyx', 'xyz', 'xzy', 'wyzx', 'wzyx')
 TAKES = {
-    (0, 0): (7, 11, 15, 19, 23, 27, 37, 41, 45, 51, 58, 64),
-    (0, 1): (13, 17, 21, 25, 29, 33, 45, 53, 60, 66, 69, 71),
-    (0, 2): (17, 21, 27, 33, 37, 39, 48, 55, 61, 66, 69, 72),
-    (1, 0): (7, 11, 15, 19, 23, 29, 33, 37, 41, 45, 51, 58),
-    (1, 1): (13, 17, 21, 25, 29, 35, 41, 47, 54, 58, 64, 67),
-    (1, 2): (15, 19, 23, 29, 35, 41, 54, 60, 66, 69, 71, 71),
-    (2, 0): (9, 11, 15, 19, 23, 29),
-    (2, 1): (13, 17, 21, 25, 29, 37),
-    (2, 2): (17, 21, 25, 29, 37, 47),
-    (2, 3): (21, 27, 33, 37, 41, 49),
+    (0, 0): (5515944, 66568),
+    (0, 1): (4281664, 9703456),
+    (0, 2): (861440, 18096258),
+    (1, 0): (5589672, 1032),
+    (1, 1): (9590080, 2360352),
+    (1, 2): (1198848, 27529248),
+    (2, 0): (21840, 0),
+    (2, 1): (283968, 0),
+    (2, 2): (8672512, 0),
+    (2, 3): (1385472, 4),
 }
-FINISH = (21, 27, 33, 37, 41, 49, 54, 60, 66, 69, 71, 72)
+FINISH = (1385472, 27529252)
 N_SUM = 7
 TICKS = 73
 ROWS_ONE = (224, 224, 64, 64, 96, 96)
@@ -247,42 +247,34 @@
             for q in range(4):
                 out_ref[pl.ds(6 * q + pos, 192, stride=24), :] = big[sum_slot, y, z, pl.ds(192 * q, 192), :]
 
-    def reached(tick, row):
-        total = jnp.int32(0)
-        for value in row:
-            total = total + jnp.where(tick >= value, 1, 0)
-        return total
+    def due(tick, words):
+        word = jnp.where(tick < 4 * STEPS, words[0], words[1])
+        place = jnp.where(tick < 4 * STEPS, tick // 2, tick - 4 * STEPS)
+        return (word >> place) & 1
 
     def run_ticks(tick, seen):
         now = []
-        for place, (key, row) in enumerate(sorted(TAKES.items())):
+        for place, (key, words) in enumerate(sorted(TAKES.items())):
             group, stage = key
-            count = reached(tick, row)
-
-            def one(unit, carry):
-                for phase in range(2):
-                    members = [i for i in (2 * group, 2 * group + 1) if placed(phase)[i][1]]
-                    if not members:
-                        continue
-
-                    @pl.when(unit // UNITS == phase)
-                    def _(phase=phase, members=members):
-                        for idx in members:
-                            stage_take(idx, stage, unit, phase)
-                            if stage + 1 < len(ORDERS[idx]):
-                                stage_send(idx, stage + 1, unit, phase)
-                return carry
-
-            lax.fori_loop(seen[place], count, one, 0)
-            now.append(count)
-        count = reached(tick, FINISH)
-
-        def last(unit, carry):
+            unit, bit = seen[place], due(tick, words)
+            for phase in range(2):
+                members = [i for i in (2 * group, 2 * group + 1) if placed(phase)[i][1]]
+                if not members:
+                    continue
+
+                @pl.when((bit == 1) & (unit // UNITS == phase))
+                def _(phase=phase, members=members, unit=unit, stage=stage):
+                    for idx in members:
+                        stage_take(idx, stage, unit, phase)
+                        if stage + 1 < len(ORDERS[idx]):
+                            stage_send(idx, stage + 1, unit, phase)
+            now.append(unit + bit)
+        unit, bit = seen[-1], due(tick, FINISH)
+
+        @pl.when(bit == 1)
+        def _():
             finish(unit)
-            return carry
-
-        lax.fori_loop(seen[-1], count, last, 0)
-        now.append(count)
+        now.append(unit + bit)
         return tuple(now)
 
     def body(tick, seen):
@@ -403,7 +395,7 @@
         def _():
             chip_sum(jnp.where(part == 3, step, step - 1))
 
-        return run_ticks(tick, seen)
+        return lax.cond((tick % 2 == 1) | (tick >= 4 * STEPS), lambda kept: run_ticks(tick, kept), lambda kept: kept, seen)
 
     lax.fori_loop(0, TICKS, body, (jnp.int32(0),) * (len(TAKES) + 1))
 

time: 180 us -> 177 us (0.983)
  Pallas kernels: 176 us -> 174 us
    pallas_call x1, Pallas kernels: 176 us -> 174 us  [per_device(): pl.pallas_call(kernel, out_shape=jax.ShapeDtypeStruct((4608, 128), f32),...]
where the time goes in v4:
time: 177 us
  Pallas kernels  174 us (98%)
  local copies, waits for them, and re-layouts  3.22 us (2%)
    pallas_call x1, Pallas kernels, per_device(): pl.pallas_call(kernel, out_shape=jax.ShapeDtypeStruct((4608, 128), f32),...  174 us

profile of v4, /device:TPU:0, one launch (start us, length us, event | category | flops | bytes accessed | tf_op | source)
XLA Modules:
  0.0 177.0 jit_solution(15289150543402361729)
XLA Ops:
  0.0 173.8 %shard_map.82 = f32[4608,128]{1,0:T(8,128)} custom-call(bf16[2048,768]{1,0:T(8,128)(2,1)} %a1_hbm.1, bf16[2048,3072]{1,0:T(8,128)(2,1)} %z1_hbm.1, bf16[2048,768]{1,0:T(8,128)(2,1)} %a2_hbm.1, bf16[2048,3072]{1,0:T(8,128)(2,1)} %z2_hbm.1, bf16[2048,768]{1,0:T(8,128)(2,1)} %g_hbm.1, bf16[768,3072]{1,0:T(8,128)(2,1)} %wi_hbm.1, bf16[3072,768]{1,0:T(8,128)(2,1)} %wo1_hbm.1, ...), custom_call_target="tpu_custom_call" | custom-call | tf_op jit(solution)/shard_map/pallas_call | solution.py:413
  173.8 3.2 %copy.10 = f32[589824]{0:T(1024)} copy(f32[589824]{0:T(1024)} %bitcast.1) | data formatting | bytes 4718592

commit v5 on v4

--- a/solution.py
+++ b/solution.py
@@ -19,22 +19,22 @@
 TILE = 1024
 ORDERS = ('yzx', 'zyx', 'xyz', 'xzy', 'wyzx', 'wzyx')
 TAKES = {
-    (0, 0): (5515944, 66568),
-    (0, 1): (4281664, 9703456),
-    (0, 2): (861440, 18096258),
-    (1, 0): (5589672, 1032),
-    (1, 1): (9590080, 2360352),
-    (1, 2): (1198848, 27529248),
-    (2, 0): (21840, 0),
-    (2, 1): (283968, 0),
-    (2, 2): (8672512, 0),
-    (2, 3): (1385472, 4),
+    (0, 0): (5393064, 2114),
+    (0, 1): (1348928, 86152),
+    (0, 2): (300288, 299278),
+    (1, 0): (5589672, 68),
+    (1, 1): (5327520, 41218),
+    (1, 2): (608896, 233736),
+    (2, 0): (9590096, 8736),
+    (2, 1): (824640, 86082),
+    (2, 2): (12883200, 463360),
+    (2, 3): (594944, 7379970),
 }
-FINISH = (1385472, 27529252)
-N_SUM = 7
-TICKS = 73
-ROWS_ONE = (224, 224, 64, 64, 96, 96)
-ROWS_TWO = (320, 320, 64, 64, 0, 0)
+FINISH = (594944, 7379970)
+N_SUM = 8
+TICKS = 71
+ROWS_ONE = (224, 224, 48, 48, 112, 112)
+ROWS_TWO = (256, 256, 48, 48, 80, 80)
 ROOT = math.sqrt(2.0 / math.pi)
 CUBE = 0.044715
 

time: 177 us -> 173 us (0.977)
  Pallas kernels: 174 us -> 169 us
    pallas_call x1, Pallas kernels: 174 us -> 169 us  [per_device(): pl.pallas_call(kernel, out_shape=jax.ShapeDtypeStruct((4608, 128), f32),...]
where the time goes in v5:
time: 173 us
  Pallas kernels  169 us (98%)
  local copies, waits for them, and re-layouts  3.22 us (2%)
    pallas_call x1, Pallas kernels, per_device(): pl.pallas_call(kernel, out_shape=jax.ShapeDtypeStruct((4608, 128), f32),...  169 us

profile of v5, /device:TPU:0, one launch (start us, length us, event | category | flops | bytes accessed | tf_op | source)
XLA Modules:
  0.0 172.7 jit_solution(15927099671090578346)
XLA Ops:
  0.0 169.4 %shard_map.82 = f32[4608,128]{1,0:T(8,128)} custom-call(bf16[2048,768]{1,0:T(8,128)(2,1)} %a1_hbm.1, bf16[2048,3072]{1,0:T(8,128)(2,1)} %z1_hbm.1, bf16[2048,768]{1,0:T(8,128)(2,1)} %a2_hbm.1, bf16[2048,3072]{1,0:T(8,128)(2,1)} %z2_hbm.1, bf16[2048,768]{1,0:T(8,128)(2,1)} %g_hbm.1, bf16[768,3072]{1,0:T(8,128)(2,1)} %wi_hbm.1, bf16[3072,768]{1,0:T(8,128)(2,1)} %wo1_hbm.1, ...), custom_call_target="tpu_custom_call" | custom-call | tf_op jit(solution)/shard_map/pallas_call | solution.py:413
  169.5 3.2 %copy.10 = f32[589824]{0:T(1024)} copy(f32[589824]{0:T(1024)} %bitcast.1) | data formatting | bytes 4718592

commit v6 on v5

--- a/solution.py
+++ b/solution.py
@@ -20,19 +20,19 @@
 ORDERS = ('yzx', 'zyx', 'xyz', 'xzy', 'wyzx', 'wzyx')
 TAKES = {
     (0, 0): (5393064, 2114),
-    (0, 1): (1348928, 86152),
-    (0, 2): (300288, 299278),
-    (1, 0): (5589672, 68),
-    (1, 1): (5327520, 41218),
-    (1, 2): (608896, 233736),
-    (2, 0): (9590096, 8736),
-    (2, 1): (824640, 86082),
-    (2, 2): (12883200, 463360),
-    (2, 3): (594944, 7379970),
+    (0, 1): (1348928, 172296),
+    (0, 2): (595200, 1123356),
+    (1, 0): (5589672, 66),
+    (1, 1): (5393056, 37128),
+    (1, 2): (1201408, 434440),
+    (2, 0): (2381136, 17441),
+    (2, 1): (2430272, 173058),
+    (2, 2): (5313792, 951300),
+    (2, 3): (1124352, 15743040),
 }
-FINISH = (594944, 7379970)
+FINISH = (1124352, 15743040)
 N_SUM = 8
-TICKS = 71
+TICKS = 72
 ROWS_ONE = (224, 224, 48, 48, 112, 112)
 ROWS_TWO = (256, 256, 48, 48, 80, 80)
 ROOT = math.sqrt(2.0 / math.pi)

time: 173 us -> 173 us (level)
  no operation moved by 1% of the time
where the time goes in v6:
time: 173 us
  Pallas kernels  170 us (98%)
  local copies, waits for them, and re-layouts  3.22 us (2%)
    pallas_call x1, Pallas kernels, per_device(): pl.pallas_call(kernel, out_shape=jax.ShapeDtypeStruct((4608, 128), f32),...  170 us

profile of v6, /device:TPU:0, one launch (start us, length us, event | category | flops | bytes accessed | tf_op | source)
XLA Modules:
  0.0 173.2 jit_solution(15012753512889822260)
XLA Ops:
  0.0 169.9 %shard_map.82 = f32[4608,128]{1,0:T(8,128)} custom-call(bf16[2048,768]{1,0:T(8,128)(2,1)} %a1_hbm.1, bf16[2048,3072]{1,0:T(8,128)(2,1)} %z1_hbm.1, bf16[2048,768]{1,0:T(8,128)(2,1)} %a2_hbm.1, bf16[2048,3072]{1,0:T(8,128)(2,1)} %z2_hbm.1, bf16[2048,768]{1,0:T(8,128)(2,1)} %g_hbm.1, bf16[768,3072]{1,0:T(8,128)(2,1)} %wi_hbm.1, bf16[3072,768]{1,0:T(8,128)(2,1)} %wo1_hbm.1, ...), custom_call_target="tpu_custom_call" | custom-call | tf_op jit(solution)/shard_map/pallas_call | solution.py:413
  169.9 3.2 %copy.10 = f32[589824]{0:T(1024)} copy(f32[589824]{0:T(1024)} %bitcast.1) | data formatting | bytes 4718592
